TPU v7x, 32 devices: a whole 2x2x4 slice. The times are simulated.
32 devices in a mesh: row: 8 (over z, x), col: 4 (over y, core).
Axes of the slice: x: 2, y: 2, z: 4, core: 2. Of those that a mesh axis runs over, the one named last changes fastest.
Arguments:
- density_first: bfloat16 [12288, 12288], P('row', 'col'), may hold values from -0.0068359375 to 0.0068359375
- density_second: bfloat16 [12288, 12288], P('row', 'col'), may hold values from -0.0068359375 to 0.0068359375
- basis: bfloat16 [64, 4096, 896], P(('row', 'col')), may hold values from -6 to 6
- tile_list: int32 [64, 7], P(('row', 'col')), may hold values from 0 to 95, as said below
- tile_count: int32 [64], P(('row', 'col')), may hold values from 5 to 7, as said below
- point_count: int32 [64], P(('row', 'col')), may hold values from 1024 to 4096, as said below
- offsets: float32 [3, 64, 4096], P(None, ('row', 'col')), may hold values from -5 to 5
- weights: float32 [64, 4096], P(('row', 'col')), may hold values from 0.05 to 1
- atom_of_point: int32 [64, 4096], P(('row', 'col')), may hold values from 0 to 1023, as said below
Outputs:
- density: float32 [2, 64, 4096], P(None, ('row', 'col'))
- moments: float32 [2, 9, 1024], replicated
Inputs may be any that keep to these rules, and one draw needn't show every extreme that they name: `tile_list`: the 7 tile numbers of each batch are 7 consecutive numbers in some order. `tile_count`: some batch has 7. `point_count`: some batch has 4096. `atom_of_point`: the points of batch g belong to atoms (g * 16 + j) mod 1024 with j from 0 to 7.
All inputs are finite; a program needn't handle non-finite values.
Results may differ from a plain program's by a relative error of at most 0.0003.
Values may be sent and summed in bfloat16 or wider, within the bound.
A program may use at most 192 MiB of HBM per device.

v0:
```python
import jax
import jax.numpy as jnp
from jax import lax
from jax.sharding import PartitionSpec as P

TILE = 128
ATOMS = 1024


def harmonics(offsets):
    first_axis = offsets[0]
    second_axis = offsets[1]
    third_axis = offsets[2]
    radius_sq = first_axis * first_axis + second_axis * second_axis + third_axis * third_axis
    return jnp.stack(
        [
            jnp.ones_like(first_axis),
            first_axis,
            second_axis,
            third_axis,
            first_axis * second_axis,
            second_axis * third_axis,
            3.0 * third_axis * third_axis - radius_sq,
            first_axis * third_axis,
            first_axis * first_axis - second_axis * second_axis,
        ]
    )


def local(
    density_first,
    density_second,
    basis,
    tile_list,
    tile_count,
    point_count,
    offsets,
    weights,
    atom_of_point,
):
    row_count = lax.axis_size("row")
    col_count = lax.axis_size("col")
    tile_size = TILE
    local_rows = density_first.shape[0] // tile_size
    local_cols = density_first.shape[1] // tile_size
    batches_dev = tile_list.shape[0]
    run_length = tile_list.shape[1]
    points = basis.shape[1]
    row_slots = -(-run_length // row_count)
    col_slots = -(-run_length // col_count)
    my_row = lax.axis_index("row")
    my_col = lax.axis_index("col")
    own_start = jnp.min(tile_list, axis=1)
    starts = lax.all_gather(own_start, ("row", "col"), axis=0, tiled=True)
    run_end = starts[:, None] + run_length
    first_row = starts + (my_row - starts) % row_count
    row_tile = first_row[:, None] + row_count * jnp.arange(row_slots, dtype=jnp.int32)[None, :]
    row_ok = row_tile < run_end
    row_local = jnp.where(row_ok, row_tile // row_count, 0)
    first_col = starts + (my_col - starts) % col_count
    col_tile = first_col[:, None] + col_count * jnp.arange(col_slots, dtype=jnp.int32)[None, :]
    col_ok = col_tile < run_end
    col_local = jnp.where(col_ok, col_tile // col_count, 0)
    wanted = row_ok[:, :, None] & col_ok[:, None, :]

    def pack_tiles(stored):
        tile_grid = stored.reshape(local_rows, tile_size, local_cols, tile_size).transpose(
            0, 2, 1, 3
        )
        picked = tile_grid[row_local[:, :, None], col_local[:, None, :]]
        picked = jnp.where(wanted[..., None, None], picked, jnp.zeros((), stored.dtype))
        return picked.reshape(
            row_count, col_count, batches_dev, row_slots, col_slots, tile_size, tile_size
        )

    outgoing_first = pack_tiles(density_first)
    outgoing_second = pack_tiles(density_second)
    flat_shape = (row_count * col_count,) + outgoing_first.shape[2:]
    flat_first = outgoing_first.reshape(flat_shape)
    flat_second = outgoing_second.reshape(flat_shape)
    moved_first, moved_second = (
        lax.all_to_all(flat_first, ("row", "col"), split_axis=0, concat_axis=0, tiled=True),
        lax.all_to_all(flat_second, ("row", "col"), split_axis=0, concat_axis=0, tiled=True),
    )
    arrived_first = moved_first.reshape(outgoing_first.shape)
    arrived_second = moved_second.reshape(outgoing_second.shape)
    offset_in_run = tile_list - own_start[:, None]
    owner_row = tile_list % row_count
    slot_row = offset_in_run // row_count
    owner_col = tile_list % col_count
    slot_col = offset_in_run // col_count
    batch_ids = jnp.arange(batches_dev, dtype=jnp.int32)[:, None, None]

    def assemble(arrived):
        blocks = arrived[
            owner_row[:, :, None],
            owner_col[:, None, :],
            batch_ids,
            slot_row[:, :, None],
            slot_col[:, None, :],
        ]
        return blocks.transpose(0, 1, 3, 2, 4).reshape(
            batches_dev, run_length * tile_size, run_length * tile_size
        )

    col_mask = jnp.arange(run_length)[None, :] < tile_count[:, None]
    col_mask = jnp.repeat(col_mask, tile_size, axis=1).astype(jnp.bfloat16)
    masked = basis * col_mask[:, None, :]
    point_mask = (jnp.arange(points)[None, :] < point_count[:, None]).astype(jnp.float32)

    def density_of(arrived):
        block = assemble(arrived)
        product = jnp.einsum("bpi,bij->bpj", masked, block, preferred_element_type=jnp.float32)
        return jnp.sum(product * masked.astype(jnp.float32), axis=2) * point_mask

    density = jnp.stack([density_of(arrived_first), density_of(arrived_second)])
    harmonic = harmonics(offsets)
    moment_terms = density[:, None] * (weights[None, None] * harmonic[None])
    flat_terms = moment_terms.reshape(2 * 9, -1)
    one_hot = (
        atom_of_point.reshape(-1)[:, None] == jnp.arange(ATOMS, dtype=jnp.int32)[None, :]
    ).astype(jnp.float32)
    partial_value = jnp.dot(
        flat_terms, one_hot, precision=lax.Precision.HIGHEST, preferred_element_type=jnp.float32
    )
    moments = lax.psum(partial_value, ("row", "col"))
    return (density, moments.reshape(2, 9, ATOMS))


def solution(mesh):
    placed = (
        P("row", "col"),
        P("row", "col"),
        P(("row", "col"), None, None),
        P(("row", "col"), None),
        P(("row", "col")),
        P(("row", "col")),
        P(None, ("row", "col"), None),
        P(("row", "col"), None),
        P(("row", "col"), None),
    )
    return jax.shard_map(
        local,
        mesh=mesh,
        in_specs=placed,
        out_specs=(P(None, ("row", "col"), None), P()),
        check_vma=False,
    )
```

profile of v0, /device:TPU:0, one launch (start us, length us, event | category | flops | bytes accessed | tf_op | source)
XLA Modules:
  0.0 516.1 jit_solution(7729851914212681637)
XLA Ops:
  7.2 0.8 fusion.11
  8.0 0.2 dynamic-update-slice
  8.2 42.0 %all-reduce = s32[64]{0:T(128)S(1)} all-reduce(s32[64]{0:T(128)S(1)} %dynamic-update-slice), channel_id=1, replica_groups=mesh['row'=8,'col'=4] {'row','col'}, use_global_device_ids=true, to_apply=%add | all-reduce | flops 64 | bytes 512
  50.2 0.1 add.135
  50.4 0.1 lt.139
  50.5 0.1 compare_select_fusion
  50.6 0.1 copy.49
  50.7 0.1 reshape.452
  50.8 9.8 %copy.68 = bf16[192,8,24,128]{3,2,1,0:T(8,128)(2,1)} copy(bf16[192,8,24,128]{3,1,2,0:T(8,128)(2,1)} %bitcast.60) | data formatting | bytes 18874368
  60.6 10.0 %copy.75 = bf16[12,128,24,128]{3,1,2,0:T(8,128)(2,1)} copy(bf16[12,128,24,128]{3,2,1,0:T(8,128)(2,1)} %bitcast.51) | data formatting | bytes 18874368 | tf_op jit(solution)/shard_map/reshape | solution.py:67
  70.6 9.9 %copy.67 = bf16[192,8,24,128]{3,2,1,0:T(8,128)(2,1)} copy(bf16[192,8,24,128]{3,1,2,0:T(8,128)(2,1)} %bitcast.61) | data formatting | bytes 18874368
  80.5 10.1 %copy.76 = bf16[12,128,24,128]{3,1,2,0:T(8,128)(2,1)} copy(bf16[12,128,24,128]{3,2,1,0:T(8,128)(2,1)} %bitcast.52) | data formatting | bytes 18874368 | tf_op jit(solution)/shard_map/reshape | solution.py:67
  90.6 6.8 %gather_fusion.2 = bf16[128,128,128]{2,1,0:T(8,128)(2,1)} fusion(bf16[12,24,128,128]{3,2,1,0:T(8,128)(2,1)} %bitcast.53, s32[128]{0:T(128)S(1)} %reshape.452), kind=kCustom, calls=%fused_computation.2 | custom fusion | bytes 8389632 | tf_op jit(solution)/shard_map/gather | solution.py:70
  97.4 6.7 %gather_fusion = bf16[128,128,128]{2,1,0:T(8,128)(2,1)} fusion(bf16[12,24,128,128]{3,2,1,0:T(8,128)(2,1)} %bitcast.54, s32[128]{0:T(128)S(1)} %reshape.452), kind=kCustom, calls=%fused_computation | custom fusion | bytes 8389632 | tf_op jit(solution)/shard_map/gather | solution.py:70
  104.2 0.1 and.74
  104.3 0.2 compare_and_fusion
  104.5 5.2 broadcast_select_fusion.1
  109.6 97.9 %all_to_all.10 = bf16[32,2,1,2,128,128]{5,4,3,1,2,0:T(8,128)(2,1)} all-to-all(bf16[32,2,1,2,128,128]{5,4,3,1,2,0:T(8,128)(2,1)S(1)} %get-tuple-element.13), channel_id=1, replica_groups=mesh['row'=8,'col'=4] {'row','col'}, dimensions={0} | all-to-all | bytes 8388608 | tf_op jit(solution)/shard_map/all_to_all | solution.py:83
  207.5 0.0 copy-start.5
  207.5 3.8 all-to-all-start
  211.3 0.5 all-reduce.3.cloned.1.call-start
  211.9 0.0 copy-done.5
  211.9 0.1 fusion.15
  212.0 0.1 or_or_fusion
  212.0 0.1 reshape.458
  212.1 0.0 copy-start.7
  212.1 0.0 copy-start.4
  212.1 0.0 copy-start.1
  212.2 0.0 copy-start.3
  212.2 19.9 %copy.46 = bf16[2,4096,896]{1,2,0:T(8,128)(2,1)} copy(bf16[2,4096,896]{2,1,0:T(8,128)(2,1)} %param.11) | data formatting | bytes 29360128 | tf_op args[2]
  232.1 0.0 copy-done.7
  232.1 0.1 compare_convert_fusion
  232.2 0.1 broadcast_bitcast_fusion
  232.2 0.0 copy-done.4
  232.3 0.0 copy-done.1
  232.4 0.1 fusion.9
  232.5 0.0 copy-done.3
  232.5 0.1 broadcast_multiply_fusion.1
  232.6 4.2 gather_fusion.3
  236.9 4.5 copy.56
  241.4 7.4 %reshape.487 = bf16[2,896,896]{2,1,0:T(8,128)(2,1)} reshape(bf16[2,7,128,7,128]{4,3,2,1,0:T(8,128)(2,1)} %copy.56) | data formatting | bytes 6422528 | tf_op jit(solution)/shard_map/reshape | solution.py:102
  248.8 56.7 %all-to-all-done = bf16[32,2,1,2,128,128]{5,4,3,1,2,0:T(8,128)(2,1)} async-done(((bf16[32,2,1,2,128,128]{5,4,3,1,2,0:T(8,128)(2,1)}), bf16[32,2,1,2,128,128]{5,4,3,1,2,0:T(8,128)(2,1)}, u32[]{:S(2)}, u32[]{:S(2)}) %all-to-all-start) | async-done | bytes 4194336 | tf_op jit(solution)/shard_map/all_to_all | solution.py:82
  305.6 4.2 gather_fusion.1
  309.8 4.5 copy.51
  314.3 0.0 copy-start
  314.3 7.6 %reshape.485 = bf16[2,896,896]{2,1,0:T(8,128)(2,1)} reshape(bf16[2,7,128,7,128]{4,3,2,1,0:T(8,128)(2,1)} %copy.51) | data formatting | bytes 6422528 | tf_op jit(solution)/shard_map/reshape | solution.py:102
  321.9 0.0 copy-done
  321.9 23.4 %fusion.2 = f32[2,4096]{1,0:T(2,128)S(1)} fusion(bf16[2,896,896]{2,1,0:T(8,128)(2,1)S(1)} %copy-done, bf16[2,4096,896]{1,2,0:T(8,128)(2,1)} %copy.46, bf16[2,896]{1,0:T(2,128)(2,1)S(1)} %bitcast.68), kind=kOutput, calls=%fused_computation.9 | convolution fusion | flops 13190029312 | bytes 17927680 | tf_op jit(solution)/shard_map/bpi,bij->bpj/dot_general | solution.py:113
  345.3 0.0 copy-start.6
  345.3 24.4 %fusion.1 = f32[2,4096]{1,0:T(2,128)S(1)} fusion(bf16[2,896,896]{2,1,0:T(8,128)(2,1)} %reshape.485, bf16[2,4096,896]{1,2,0:T(8,128)(2,1)} %copy.46, bf16[2,896]{1,0:T(2,128)(2,1)S(1)} %bitcast.69), kind=kOutput, calls=%fused_computation.8 | convolution fusion | flops 13190029312 | bytes 17927680 | tf_op jit(solution)/shard_map/bpi,bij->bpj/dot_general | solution.py:113
  369.8 0.0 copy-done.6
  369.8 0.1 bitcast_select_fusion.1
  369.9 0.0 copy-start.2
  369.9 0.2 broadcast_multiply_fusion
  370.2 0.4 pad.4
  370.5 0.5 copy.69
  371.0 10.5 %fusion = f32[18,1024]{1,0:T(8,128)S(1)} fusion(f32[18,8192]{1,0:T(8,128)S(1)} %bitcast.64, s32[8192]{0:T(1024)S(1)} %bitcast.66), kind=kOutput, calls=%fused_computation.7 | convolution fusion | flops 1820327936 | bytes 696320 | tf_op jit(solution)/shard_map/dot_general | solution.py:123
  381.5 0.0 copy-done.2
  381.5 0.7 reshape.449
  382.2 0.0 all-reduce.3.cloned.1.call-update
  382.2 125.1 %all-reduce.3.cloned.1.call-done = f32[2,9,1024]{2,1,0:T(8,128)} async-done(((f32[2,9,1024]{2,1,0:T(8,128)}), f32[2,9,1024]{2,1,0:T(8,128)}) %all-reduce.3.cloned.1.call-update) | async-done | bytes 73744 | tf_op jit(solution)/shard_map/psum | solution.py:126
  507.3 1.6 copy.59
  (17 shorter events, 0.2 us)
Async XLA Ops:
  207.5 4.3 copy-start.5
  207.5 98.0 %all-to-all-start = ((bf16[32,2,1,2,128,128]{5,4,3,1,2,0:T(8,128)(2,1)}), bf16[32,2,1,2,128,128]{5,4,3,1,2,0:T(8,128)(2,1)}, u32[]{:S(2)}, u32[]{:S(2)}) async-start(bf16[32,2,1,2,128,128]{5,4,3,1,2,0:T(8,128)(2,1)} %get-tuple-element.12), calls=%async_computation | async-start | bytes 8388608 | tf_op jit(solution)/shard_map/all_to_all | solution.py:82
  211.3 295.9 %all-reduce.3.cloned.1.call-start = ((), (), s32[]{:S(2)}) async-start(), calls=%async_computation.2 | async-start | bytes 262144 | tf_op jit(solution)/shard_map/psum | solution.py:126
  212.1 20.0 %copy-start.7 = (s32[2]{0:T(128)S(1)}, s32[2]{0:T(128)}, u32[]{:S(2)}) copy-start(s32[2]{0:T(128)} %param.13) | copy-start | bytes 28
  212.1 20.1 %copy-start.4 = (s32[2,4096]{1,0:T(2,128)S(1)}, s32[2,4096]{1,0:T(2,128)}, u32[]{:S(2)}) copy-start(s32[2,4096]{1,0:T(2,128)} %param.17) | copy-start | bytes 98308
  212.1 20.1 %copy-start.1 = (f32[3,2,4096]{2,1,0:T(2,128)S(1)}, f32[3,2,4096]{2,1,0:T(2,128)}, u32[]{:S(2)}) copy-start(f32[3,2,4096]{2,1,0:T(2,128)} %param.15) | copy-start | bytes 294916
  212.2 20.3 %copy-start.3 = (f32[2,4096]{1,0:T(2,128)S(1)}, f32[2,4096]{1,0:T(2,128)}, u32[]{:S(2)}) copy-start(f32[2,4096]{1,0:T(2,128)} %param.16) | copy-start | bytes 98308
  314.3 7.6 %copy-start = (bf16[2,896,896]{2,1,0:T(8,128)(2,1)S(1)}, bf16[2,896,896]{2,1,0:T(8,128)(2,1)}, u32[]{:S(2)}) copy-start(bf16[2,896,896]{2,1,0:T(8,128)(2,1)} %reshape.487) | copy-start | bytes 9633796
  345.3 24.5 %copy-start.6 = (s32[2]{0:T(128)S(1)}, s32[2]{0:T(128)}, u32[]{:S(2)}) copy-start(s32[2]{0:T(128)} %param.14) | copy-start | bytes 28
  369.9 11.6 %copy-start.2 = (f32[2,2,4096]{2,1,0:T(2,128)}, f32[2,2,4096]{2,1,0:T(2,128)S(1)}, u32[]{:S(2)}) copy-start(f32[2,2,4096]{2,1,0:T(2,128)S(1)} %pad_maximum_fusion) | copy-start | bytes 196612
Sparse Core Ops, SparseCore 0:
  382.3 124.9 all-reduce.2
where the time goes:
time: 525 us; the launch traced here: 516 us
  waiting for transfers between devices  182 us (35%)
  blocking collectives  140 us (27%)
  local copies, waits for them, and re-layouts  110 us (21%)
  matrix products  58.4 us (11%)
  between operations  14.7 us (3%)
  other arithmetic  7.15 us (1%)
    psum x1, waiting for transfers between devices, local(): moments = lax.psum(partial_value, ('row', 'col'))  125 us
    all_to_all x1, blocking collectives, local(): lax.all_to_all(flat_second, ('row', 'col'), split_axis=0, concat_axis=0,...  97.9 us
    all_to_all x1, waiting for transfers between devices, local(): lax.all_to_all(flat_first, ('row', 'col'), split_axis=0, concat_axis=0, t...  56.7 us
    dot_general x2, matrix products, density_of(): jnp.einsum('bpi,bij->bpj', masked, block, preferred_element_type=jnp.floa...  47.8 us
    unnamed x29, local copies, waits for them, and re-layouts  42.4 us
    unnamed x1, blocking collectives  42 us
    reshape x2, local copies, waits for them, and re-layouts, pack_tiles(): stored.reshape(local_rows, tile_size, local_cols, tile_size)  20.1 us
    reshape x2, local copies, waits for them, and re-layouts, assemble(): blocks.transpose(0, 1, 3, 2, 4)  15 us
  transfers between devices with their start and end apart: 2, of which 2 were waited for; matrix products, arithmetic and copies ran while one was open for 7% of the time, Pallas kernels for 0%

commit v1 on v0

--- a/solution.py
+++ b/solution.py
@@ -123,7 +123,9 @@
     partial_value = jnp.dot(
         flat_terms, one_hot, precision=lax.Precision.HIGHEST, preferred_element_type=jnp.float32
     )
-    moments = lax.psum(partial_value, ("row", "col"))
+    moments = partial_value
+    for name in ("col", "row"):
+        moments = lax.psum(moments, name)
     return (density, moments.reshape(2, 9, ATOMS))
 
 

time: 525 us -> 506 us (0.964)
  waiting for transfers between devices: 182 us -> 161 us
    psum x1 -> x2, waiting for transfers between devices: 125 us -> 105 us  [local(): moments = lax.psum(moments, name)]
  transfers between devices with their start and end apart: 2 -> 3, of which waited for: 2 -> 3; matrix products, arithmetic and copies ran while one was open for 7% -> 7% of each run, Pallas kernels for 0% -> 0%
where the time goes in v1:
time: 506 us; the launch traced here: 497 us
  waiting for transfers between devices  161 us (32%)
  blocking collectives  140 us (28%)
  local copies, waits for them, and re-layouts  111 us (22%)
  matrix products  59 us (12%)
  between operations  14.7 us (3%)
  other arithmetic  7.15 us (1%)
    psum x2, waiting for transfers between devices, local(): moments = lax.psum(moments, name)  105 us
    all_to_all x1, blocking collectives, local(): lax.all_to_all(flat_second, ('row', 'col'), split_axis=0, concat_axis=0,...  97.9 us
    all_to_all x1, waiting for transfers between devices, local(): lax.all_to_all(flat_first, ('row', 'col'), split_axis=0, concat_axis=0, t...  56.7 us
    dot_general x2, matrix products, density_of(): jnp.einsum('bpi,bij->bpj', masked, block, preferred_element_type=jnp.floa...  47.8 us
    unnamed x29, local copies, waits for them, and re-layouts  42.4 us
    unnamed x1, blocking collectives  42 us
    reshape x2, local copies, waits for them, and re-layouts, pack_tiles(): stored.reshape(local_rows, tile_size, local_cols, tile_size)  20.1 us
    reshape x2, local copies, waits for them, and re-layouts, assemble(): blocks.transpose(0, 1, 3, 2, 4)  15 us
  transfers between devices with their start and end apart: 3, of which 3 were waited for; matrix products, arithmetic and copies ran while one was open for 7% of the time, Pallas kernels for 0%

profile of v1, /device:TPU:0, one launch (start us, length us, event | category | flops | bytes accessed | tf_op | source)
XLA Modules:
  0.0 497.2 jit_solution(14238402267019507991)
XLA Ops:
  7.2 0.8 fusion.11
  8.0 0.2 dynamic-update-slice
  8.2 42.0 %all-reduce = s32[64]{0:T(128)S(1)} all-reduce(s32[64]{0:T(128)S(1)} %dynamic-update-slice), channel_id=1, replica_groups=mesh['row'=8,'col'=4] {'row','col'}, use_global_device_ids=true, to_apply=%add | all-reduce | flops 64 | bytes 512
  50.2 0.1 add.137
  50.3 0.1 lt.139
  50.5 0.1 compare_select_fusion
  50.6 0.1 copy.49
  50.7 0.1 reshape.452
  50.8 9.8 %copy.68 = bf16[192,8,24,128]{3,2,1,0:T(8,128)(2,1)} copy(bf16[192,8,24,128]{3,1,2,0:T(8,128)(2,1)} %bitcast.60) | data formatting | bytes 18874368
  60.6 10.0 %copy.75 = bf16[12,128,24,128]{3,1,2,0:T(8,128)(2,1)} copy(bf16[12,128,24,128]{3,2,1,0:T(8,128)(2,1)} %bitcast.51) | data formatting | bytes 18874368 | tf_op jit(solution)/shard_map/reshape | solution.py:67
  70.6 9.9 %copy.67 = bf16[192,8,24,128]{3,2,1,0:T(8,128)(2,1)} copy(bf16[192,8,24,128]{3,1,2,0:T(8,128)(2,1)} %bitcast.61) | data formatting | bytes 18874368
  80.5 10.1 %copy.76 = bf16[12,128,24,128]{3,1,2,0:T(8,128)(2,1)} copy(bf16[12,128,24,128]{3,2,1,0:T(8,128)(2,1)} %bitcast.52) | data formatting | bytes 18874368 | tf_op jit(solution)/shard_map/reshape | solution.py:67
  90.6 6.8 %gather_fusion.2 = bf16[128,128,128]{2,1,0:T(8,128)(2,1)} fusion(bf16[12,24,128,128]{3,2,1,0:T(8,128)(2,1)} %bitcast.53, s32[128]{0:T(128)S(1)} %reshape.452), kind=kCustom, calls=%fused_computation.2 | custom fusion | bytes 8389632 | tf_op jit(solution)/shard_map/gather | solution.py:70
  97.4 6.7 %gather_fusion = bf16[128,128,128]{2,1,0:T(8,128)(2,1)} fusion(bf16[12,24,128,128]{3,2,1,0:T(8,128)(2,1)} %bitcast.54, s32[128]{0:T(128)S(1)} %reshape.452), kind=kCustom, calls=%fused_computation | custom fusion | bytes 8389632 | tf_op jit(solution)/shard_map/gather | solution.py:70
  104.2 0.1 and.74
  104.3 0.2 compare_and_fusion
  104.5 5.2 %broadcast_select_fusion.1 = (bf16[32,2,1,2,128,128]{5,4,3,1,2,0:T(8,128)(2,1)}, bf16[32,2,1,2,128,128]{5,4,3,1,2,0:T(8,128)(2,1)S(1)}) fusion(bf16[32,2,1,2,128,128]{5,4,3,1,2,0:T(8,128)(2,1)} %bitcast.56, pred[32,2,2]{2,1,0:T(4,128)(4,1)S(1)} %compare_and_fusion, bf16[32,2,1,2,128,128]{5,4,3,1,2,0:T(8,128)(2,1)} %bitcast.55), kind=kLoop, calls=%fused_computation.18 | loop fusion | flops 4194304 | bytes 16777344 | tf_op jit(solution)/shard_map/jit(_where)/select_n | solution.py:71
  109.6 97.9 %all_to_all.10 = bf16[32,2,1,2,128,128]{5,4,3,1,2,0:T(8,128)(2,1)} all-to-all(bf16[32,2,1,2,128,128]{5,4,3,1,2,0:T(8,128)(2,1)S(1)} %get-tuple-element.13), channel_id=1, replica_groups=mesh['row'=8,'col'=4] {'row','col'}, dimensions={0} | all-to-all | bytes 8388608 | tf_op jit(solution)/shard_map/all_to_all | solution.py:83
  207.5 0.0 copy-start.5
  207.5 3.8 all-to-all-start
  211.3 0.5 all-reduce.4.cloned.1.call-start
  211.9 0.0 copy-done.5
  211.9 0.1 fusion.15
  211.9 0.1 or_or_fusion
  212.0 0.1 reshape.458
  212.1 0.0 copy-start.7
  212.1 0.0 copy-start.4
  212.1 0.0 copy-start.1
  212.1 0.0 copy-start.3
  212.2 19.9 %copy.46 = bf16[2,4096,896]{1,2,0:T(8,128)(2,1)} copy(bf16[2,4096,896]{2,1,0:T(8,128)(2,1)} %param.11) | data formatting | bytes 29360128 | tf_op args[2]
  232.1 0.0 copy-done.7
  232.1 0.1 compare_convert_fusion
  232.2 0.1 broadcast_bitcast_fusion
  232.2 0.0 copy-done.4
  232.3 0.0 copy-done.1
  232.4 0.1 fusion.9
  232.5 0.0 copy-done.3
  232.5 0.1 broadcast_multiply_fusion.1
  232.6 4.2 gather_fusion.3
  236.9 4.5 copy.56
  241.4 7.4 %reshape.487 = bf16[2,896,896]{2,1,0:T(8,128)(2,1)} reshape(bf16[2,7,128,7,128]{4,3,2,1,0:T(8,128)(2,1)} %copy.56) | data formatting | bytes 6422528 | tf_op jit(solution)/shard_map/reshape | solution.py:102
  248.8 56.7 %all-to-all-done = bf16[32,2,1,2,128,128]{5,4,3,1,2,0:T(8,128)(2,1)} async-done(((bf16[32,2,1,2,128,128]{5,4,3,1,2,0:T(8,128)(2,1)}), bf16[32,2,1,2,128,128]{5,4,3,1,2,0:T(8,128)(2,1)}, u32[]{:S(2)}, u32[]{:S(2)}) %all-to-all-start) | async-done | bytes 4194336 | tf_op jit(solution)/shard_map/all_to_all | solution.py:82
  305.6 4.2 gather_fusion.1
  309.8 4.5 copy.51
  314.3 7.6 %reshape.485 = bf16[2,896,896]{2,1,0:T(8,128)(2,1)} reshape(bf16[2,7,128,7,128]{4,3,2,1,0:T(8,128)(2,1)} %copy.51) | data formatting | bytes 6422528 | tf_op jit(solution)/shard_map/reshape | solution.py:102
  321.9 0.0 copy-done
  321.9 23.4 %fusion.2 = f32[2,4096]{1,0:T(2,128)S(1)} fusion(bf16[2,896,896]{2,1,0:T(8,128)(2,1)S(1)} %copy-done, bf16[2,4096,896]{1,2,0:T(8,128)(2,1)} %copy.46, bf16[2,896]{1,0:T(2,128)(2,1)S(1)} %bitcast.68), kind=kOutput, calls=%fused_computation.9 | convolution fusion | flops 13190029312 | bytes 17927680 | tf_op jit(solution)/shard_map/bpi,bij->bpj/dot_general | solution.py:113
  345.3 0.0 copy-start.6
  345.3 24.4 %fusion.1 = f32[2,4096]{1,0:T(2,128)S(1)} fusion(bf16[2,896,896]{2,1,0:T(8,128)(2,1)} %reshape.485, bf16[2,4096,896]{1,2,0:T(8,128)(2,1)} %copy.46, bf16[2,896]{1,0:T(2,128)(2,1)S(1)} %bitcast.69), kind=kOutput, calls=%fused_computation.8 | convolution fusion | flops 13190029312 | bytes 17927680 | tf_op jit(solution)/shard_map/bpi,bij->bpj/dot_general | solution.py:113
  369.7 0.0 copy-done.6
  369.7 0.1 bitcast_select_fusion.1
  369.9 0.0 copy-start.2
  369.9 0.2 broadcast_multiply_fusion
  370.1 0.4 pad.4
  370.5 0.5 copy.69
  371.0 11.2 %fusion = f32[18,1024]{1,0:T(8,128)} fusion(f32[18,8192]{1,0:T(8,128)S(1)} %bitcast.64, s32[8192]{0:T(1024)S(1)} %bitcast.66), kind=kOutput, calls=%fused_computation.7 | convolution fusion | flops 1820327936 | bytes 696320 | tf_op jit(solution)/shard_map/dot_general | solution.py:123
  382.1 0.0 copy-done.2
  382.1 0.0 all-reduce.4.cloned.1.call-update
  382.2 0.0 all-reduce.6.cloned.1.call-start
  382.2 32.3 %all-reduce.4.cloned.1.call-done = f32[18,1024]{1,0:T(8,128)} async-done(((f32[18,1024]{1,0:T(8,128)}), f32[18,1024]{1,0:T(8,128)}) %all-reduce.4.cloned.1.call-update) | async-done | bytes 73744 | tf_op jit(solution)/shard_map/psum | solution.py:128
  414.5 1.6 reshape.449
  416.0 0.0 all-reduce.6.cloned.1.call-update
  416.1 72.3 %all-reduce.6.cloned.1.call-done = f32[2,9,1024]{2,1,0:T(8,128)} async-done(((f32[2,9,1024]{2,1,0:T(8,128)}), f32[2,9,1024]{2,1,0:T(8,128)}) %all-reduce.6.cloned.1.call-update) | async-done | bytes 73744 | tf_op jit(solution)/shard_map/psum | solution.py:128
  488.3 1.6 copy.59
  (18 shorter events, 0.2 us)
Async XLA Ops:
  207.5 4.3 copy-start.5
  207.5 98.0 %all-to-all-start = ((bf16[32,2,1,2,128,128]{5,4,3,1,2,0:T(8,128)(2,1)}), bf16[32,2,1,2,128,128]{5,4,3,1,2,0:T(8,128)(2,1)}, u32[]{:S(2)}, u32[]{:S(2)}) async-start(bf16[32,2,1,2,128,128]{5,4,3,1,2,0:T(8,128)(2,1)} %get-tuple-element.12), calls=%async_computation | async-start | bytes 8388608 | tf_op jit(solution)/shard_map/all_to_all | solution.py:82
  211.3 203.1 %all-reduce.4.cloned.1.call-start = ((), (), s32[]{:S(2)}) async-start(), calls=%async_computation.2 | async-start | bytes 196608 | tf_op jit(solution)/shard_map/psum | solution.py:128
  212.1 20.0 %copy-start.7 = (s32[2]{0:T(128)S(1)}, s32[2]{0:T(128)}, u32[]{:S(2)}) copy-start(s32[2]{0:T(128)} %param.13) | copy-start | bytes 28
  212.1 20.1 %copy-start.4 = (s32[2,4096]{1,0:T(2,128)S(1)}, s32[2,4096]{1,0:T(2,128)}, u32[]{:S(2)}) copy-start(s32[2,4096]{1,0:T(2,128)} %param.17) | copy-start | bytes 98308
  212.1 20.1 %copy-start.1 = (f32[3,2,4096]{2,1,0:T(2,128)S(1)}, f32[3,2,4096]{2,1,0:T(2,128)}, u32[]{:S(2)}) copy-start(f32[3,2,4096]{2,1,0:T(2,128)} %param.15) | copy-start | bytes 294916
  212.1 20.3 %copy-start.3 = (f32[2,4096]{1,0:T(2,128)S(1)}, f32[2,4096]{1,0:T(2,128)}, u32[]{:S(2)}) copy-start(f32[2,4096]{1,0:T(2,128)} %param.16) | copy-start | bytes 98308
  314.3 7.6 %copy-start = (bf16[2,896,896]{2,1,0:T(8,128)(2,1)S(1)}, bf16[2,896,896]{2,1,0:T(8,128)(2,1)}, u32[]{:S(2)}) copy-start(bf16[2,896,896]{2,1,0:T(8,128)(2,1)} %reshape.487) | copy-start | bytes 9633796
  345.3 24.4 %copy-start.6 = (s32[2]{0:T(128)S(1)}, s32[2]{0:T(128)}, u32[]{:S(2)}) copy-start(s32[2]{0:T(128)} %param.14) | copy-start | bytes 28
  369.9 12.3 %copy-start.2 = (f32[2,2,4096]{2,1,0:T(2,128)}, f32[2,2,4096]{2,1,0:T(2,128)S(1)}, u32[]{:S(2)}) copy-start(f32[2,2,4096]{2,1,0:T(2,128)S(1)} %pad_maximum_fusion) | copy-start | bytes 196612
  382.2 106.2 %all-reduce.6.cloned.1.call-start = ((), (), s32[]{:S(2)}) async-start(), calls=%async_computation.3 | async-start | bytes 262144 | tf_op jit(solution)/shard_map/psum | solution.py:128
Sparse Core Ops, SparseCore 0:
  382.3 32.1 all-reduce.3
  417.8 70.4 all-reduce.5
